TPU v7x, 32 devices: a whole 2x2x4 slice. The times are simulated.
32 devices in a mesh: grp: 2 (over y), tok: 4 (over z), feat: 4 (over x, core).
Axes of the slice: x: 2, y: 2, z: 4, core: 2. Of those that a mesh axis runs over, the one named last changes fastest.
Arguments:
- acts: bfloat16 [6144, 28672], P(('grp', 'tok'), 'feat'), parts along dimension 0, may hold values from -6 to 6
- grads: bfloat16 [6144, 8192], P(('grp', 'tok'), 'feat'), parts along dimension 0, may hold values from -6 to 6
- proj_in: bfloat16 [28672, 512], P('feat'), may hold values from -0.03125 to 0.03125
- proj_out: bfloat16 [8192, 512], P('feat'), may hold values from -0.0625 to 0.0625
- doc_lengths: int32 [8], P('grp'), parts along dimension 0, may hold values from 1 to 1536, 3072 in all
- doc_owner: int32 [8], P('grp'), parts along dimension 0, may hold values from 0 to 3, as said below
Outputs:
- doc_grads: float32 [8, 512, 512], P(('grp', 'tok'), 'feat'), parts along dimension 0
There are 2 independent parts, one for each index of `grp`. A program takes and returns all parts, laid end to end along the dimension named above; an argument that names none is the same for every part. Nothing has to cross between parts.
Inputs may be any that keep to these rules, and one draw needn't show every extreme that they name: `doc_lengths`: the lengths sum to 3072; the largest is exactly 1536. `doc_owner`: every index along tok owns exactly 1 documents.
All inputs are finite; a program needn't handle non-finite values.
Results may differ from a plain program's by a relative error of at most 0.0043.
Values may be sent and summed in bfloat16 or wider, within the bound.
No kernel may reach another device: no remote copies, remote signals or barrier semaphores. Data moves between devices by JAX's collectives and lax.ppermute only.
A program may use at most 64 MiB of HBM per device.

v0:
```python
import jax
import jax.numpy as jnp
from jax import lax
from jax.sharding import PartitionSpec as P


def outer_sum(weight_cols, low_out, low_in):
    width = weight_cols.shape[1]
    row_share = low_out.shape[1]
    weighted = (low_out[:, None, :] * weight_cols[:, :, None]).reshape(
        low_out.shape[0], width * row_share
    )
    product = lax.dot_general(
        weighted, low_in, (((0,), (0,)), ((), ())), preferred_element_type=jnp.float32
    )
    return product.reshape(width, row_share, low_in.shape[1])


def shards(acts, grads, proj_in, proj_out, doc_lengths, doc_owner):
    tok_rows = acts.shape[0]
    doc_count = doc_lengths.shape[0]
    slot_count = doc_count // lax.axis_size("tok")
    part_in = jnp.dot(acts, proj_in, preferred_element_type=jnp.float32)
    part_out = jnp.dot(grads, proj_out, preferred_element_type=jnp.float32)
    full_in = lax.psum(part_in, "feat")
    grad_part = lax.psum_scatter(part_out, "feat", scatter_dimension=1, tiled=True)
    in_low = full_in.astype(jnp.bfloat16)
    out_low = grad_part.astype(jnp.bfloat16)
    doc_ends = jnp.cumsum(doc_lengths)
    doc_starts = doc_ends - doc_lengths
    doc_index = jnp.arange(doc_count, dtype=jnp.int32)
    same_owner = doc_owner[:, None] == doc_owner[None, :]
    earlier = doc_index[:, None] < doc_index[None, :]
    slot_rank = jnp.sum((same_owner & earlier).astype(jnp.int32), axis=0)
    target = doc_owner * slot_count + slot_rank
    matches = target[:, None] == doc_index[None, :]
    routing = matches.astype(jnp.bfloat16)
    own_first = lax.axis_index("tok") * slot_count
    position = lax.axis_index("tok") * tok_rows + jnp.arange(tok_rows, dtype=jnp.int32)
    member = (
        (position[:, None] >= doc_starts[None, :]) & (position[:, None] < doc_ends[None, :])
    ).astype(jnp.bfloat16)
    all_weights = jnp.dot(member, routing, preferred_element_type=jnp.float32).astype(jnp.bfloat16)
    totals = lax.psum_scatter(
        outer_sum(all_weights, out_low, in_low), "tok", scatter_dimension=0, tiled=True
    )
    slot_lengths = jnp.sum(jnp.where(matches, doc_lengths[:, None], 0), axis=0)
    own_lengths = lax.dynamic_slice_in_dim(slot_lengths, own_first, slot_count, 0)
    scaling = lax.rsqrt(own_lengths.astype(jnp.float32))
    return totals * scaling[:, None, None]


def solution(mesh):
    in_specs = (
        P(("grp", "tok"), "feat"),
        P(("grp", "tok"), "feat"),
        P("feat", None),
        P("feat", None),
        P("grp"),
        P("grp"),
    )
    out_specs = P(("grp", "tok"), "feat", None)
    return jax.shard_map(shards, mesh=mesh, in_specs=in_specs, out_specs=out_specs, check_vma=False)
```

profile of v0, /device:TPU:0, one launch (start us, length us, event | category | flops | bytes accessed | tf_op | source)
XLA Modules:
  0.0 109.7 jit_solution(2129140301364226923)
XLA Ops:
  6.5 0.0 copy-start
  6.5 0.0 copy-start.1
  6.5 0.0 reduce-scatter.3.cloned.1.call-start
  6.5 1.9 %copy-done = bf16[768,2048]{1,0:T(8,128)(2,1)S(1)} copy-done((bf16[768,2048]{1,0:T(8,128)(2,1)S(1)}, bf16[768,2048]{1,0:T(8,128)(2,1)}, u32[]{:S(2)}) %copy-start) | copy-done | bytes 3145752
  8.4 4.5 %fusion.15 = f32[768,512]{1,0:T(8,128)} fusion(bf16[768,2048]{1,0:T(8,128)(2,1)S(1)} %copy-done, bf16[2048,512]{1,0:T(8,128)(2,1)} %param.9), kind=kOutput, calls=%fused_computation.23 | convolution fusion | flops 1610612736 | bytes 6815744 | tf_op jit(solution)/shard_map/dot_general | solution.py:24
  13.0 0.0 reduce-scatter.3.cloned.1.call-update
  13.0 0.0 reduce-scatter.5.cloned.1.call-start
  13.0 0.0 copy-done.1
  13.1 0.1 convert_reduce_fusion
  13.1 0.0 copy-start.2
  13.1 11.6 %fusion.16 = f32[768,512]{1,0:T(8,128)} fusion(bf16[768,7168]{1,0:T(8,128)(2,1)} %param.6, bf16[7168,512]{1,0:T(8,128)(2,1)} %param.8), kind=kOutput, calls=%fused_computation.24 | convolution fusion | flops 5637144576 | bytes 19922944 | tf_op jit(solution)/shard_map/dot_general | solution.py:23
  24.8 0.0 copy-done.2
  24.8 0.2 reduce-window.8
  25.0 0.3 convolution_convert_fusion
  25.2 43.7 %all-reduce.1 = bf16[768,512]{1,0:T(8,128)(2,1)} all-reduce(f32[768,512]{1,0:T(8,128)} %fusion.16), channel_id=1, replica_groups=mesh['grp'=2,'tok'=4,'feat'=4] {'feat'}, use_global_device_ids=true, to_apply=%region_3.4 | all-reduce | flops 393216 | bytes 2359296 | tf_op jit(solution)/shard_map/psum | solution.py:25
  68.9 0.0 reduce-scatter.3.cloned.1.call-done
  68.9 1.0 convert_element_type.17
  70.0 0.1 copy.9
  70.1 2.7 %fusion = f32[4,128,512]{2,1,0:T(8,128)} fusion(bf16[768,512]{1,0:T(8,128)(2,1)} %all-reduce.1, bf16[768,4]{0,1:T(4,128)(2,1)S(1)} %convolution_convert_fusion, bf16[768,128]{0,1:T(8,128)(2,1)S(1)} %copy.9), kind=kOutput, calls=%fused_computation.1 | convolution fusion | flops 403046400 | bytes 2037760 | tf_op jit(solution)/shard_map/dot_general | solution.py:13
  72.8 0.0 reduce-scatter.5.cloned.1.call-update
  72.8 0.1 select_reduce_fusion
  72.9 0.6 dynamic_slice.3
  74.2 26.9 %reduce-scatter.5.cloned.1.call-done = f32[1,128,512]{2,1,0:T(8,128)} async-done(((f32[4,128,512]{2,1,0:T(8,128)}), f32[1,128,512]{2,1,0:T(8,128)}) %reduce-scatter.5.cloned.1.call-update) | async-done | bytes 262160 | tf_op jit(solution)/shard_map/reduce_scatter | solution.py:44
  101.1 1.7 %broadcast_multiply_fusion = f32[1,128,512]{2,1,0:T(8,128)} fusion(f32[1,128,512]{2,1,0:T(8,128)} %reduce-scatter.5.cloned.1.call-done, f32[]{:T(128)} %bitcast.6), kind=kLoop, calls=%fused_computation.8 | loop fusion | flops 65536 | bytes 524292 | tf_op jit(solution)/shard_map/mul | solution.py:50
  (3 shorter events, 0.0 us)
Async XLA Ops:
  6.5 1.9 %copy-start = (bf16[768,2048]{1,0:T(8,128)(2,1)S(1)}, bf16[768,2048]{1,0:T(8,128)(2,1)}, u32[]{:S(2)}) copy-start(bf16[768,2048]{1,0:T(8,128)(2,1)} %param.7) | copy-start | bytes 9437188
  6.5 6.5 %copy-start.1 = (s32[4]{0:T(128)S(1)}, s32[4]{0:T(128)}, u32[]{:S(2)}) copy-start(s32[4]{0:T(128)} %param.11) | copy-start | bytes 52
  6.5 62.4 %reduce-scatter.3.cloned.1.call-start = ((), (), s32[]{:S(2)}) async-start(), calls=%async_computation.2 | async-start | bytes 1966080 | tf_op jit(solution)/shard_map/reduce_scatter | solution.py:26
  13.0 88.2 %reduce-scatter.5.cloned.1.call-start = ((), (), s32[]{:S(2)}) async-start(), calls=%async_computation.3 | async-start | bytes 1310720 | tf_op jit(solution)/shard_map/reduce_scatter | solution.py:44
  13.1 11.6 %copy-start.2 = (s32[4]{0:T(128)S(1)}, s32[4]{0:T(128)}, u32[]{:S(2)}) copy-start(s32[4]{0:T(128)} %param.10) | copy-start | bytes 52
Sparse Core Ops, SparseCore 0:
  13.1 39.2 reduce-scatter.2
  73.0 28.1 reduce-scatter.4
where the time goes:
time: 110 us
  blocking collectives  43.7 us (40%)
  waiting for transfers between devices  27 us (25%)
  matrix products  19.1 us (17%)
  between operations  14.1 us (13%)
  other arithmetic  3.05 us (3%)
  local copies, waits for them, and re-layouts  2.62 us (2%)
    psum x1, blocking collectives, shards(): full_in = lax.psum(part_in, 'feat')  43.7 us
    reduce_scatter x1, waiting for transfers between devices, shards(): lax.psum_scatter(outer_sum(all_weights, out_low, in_low), 'tok', scatter_...  26.9 us
    dot_general x1, matrix products, shards(): part_in = jnp.dot(acts, proj_in, preferred_element_type=jnp.float32)  11.6 us
    dot_general x1, matrix products, shards(): part_out = jnp.dot(grads, proj_out, preferred_element_type=jnp.float32)  4.54 us
    dot_general x1, matrix products, outer_sum(): lax.dot_general(weighted, low_in, (((0,), (0,)), ((), ())), preferred_ele...  2.7 us
  transfers between devices with their start and end apart: 2, of which 1 were waited for; matrix products, arithmetic and copies ran while one was open for 12% of the time, Pallas kernels for 0%

commit v1 on v0

--- a/solution.py
+++ b/solution.py
@@ -22,7 +22,9 @@
     slot_count = doc_count // lax.axis_size("tok")
     part_in = jnp.dot(acts, proj_in, preferred_element_type=jnp.float32)
     part_out = jnp.dot(grads, proj_out, preferred_element_type=jnp.float32)
-    full_in = lax.psum(part_in, "feat")
+    full_in = part_in
+    for hop in (1, 2):
+        full_in = full_in + lax.ppermute(full_in, "feat", [(dev, dev ^ hop) for dev in range(4)])
     grad_part = lax.psum_scatter(part_out, "feat", scatter_dimension=1, tiled=True)
     in_low = full_in.astype(jnp.bfloat16)
     out_low = grad_part.astype(jnp.bfloat16)

time: 110 us -> 116 us (1.055)
  waiting for transfers between devices: 27 us -> 72.2 us
  blocking collectives: 43.7 us -> 0 us
  starting transfers between devices: 0.04 us -> 3.44 us
  other arithmetic: 3.05 us -> 4.55 us
    psum x1 -> x0, blocking collectives: 43.7 us -> none  [shards(): full_in = lax.psum(part_in, 'feat')]
    ppermute x0 -> x2, waiting for transfers between devices: none -> 24.6 us  [shards(): lax.ppermute(full_in, 'feat', [(dev, dev ^ hop) for dev in range(4)])]
    reduce_scatter x1, waiting for transfers between devices: 0.01 us -> 20.1 us  [shards(): lax.psum_scatter(part_out, 'feat', scatter_dimension=1, tiled=True)]
    ppermute x0 -> x2, starting transfers between devices: none -> 3.39 us  [shards(): lax.ppermute(full_in, 'feat', [(dev, dev ^ hop) for dev in range(4)])]
    add x0 -> x1, other arithmetic: none -> 1.49 us  [shards(): full_in + lax.ppermute(full_in, 'feat', [(dev, dev ^ hop) for dev in rang...]
  transfers between devices with their start and end apart: 2 -> 4, of which waited for: 1 -> 4; matrix products, arithmetic and copies ran while one was open for 12% -> 13% of each run, Pallas kernels for 0% -> 0%
where the time goes in v1:
time: 116 us
  waiting for transfers between devices  72.2 us (62%)
  matrix products  19 us (16%)
  between operations  14.1 us (12%)
  other arithmetic  4.55 us (4%)
  starting transfers between devices  3.44 us (3%)
  local copies, waits for them, and re-layouts  2.63 us (2%)
    reduce_scatter x1, waiting for transfers between devices, shards(): lax.psum_scatter(outer_sum(all_weights, out_low, in_low), 'tok', scatter_...  27.4 us
    ppermute x2, waiting for transfers between devices, shards(): lax.ppermute(full_in, 'feat', [(dev, dev ^ hop) for dev in range(4)])  24.6 us
    reduce_scatter x1, waiting for transfers between devices, shards(): lax.psum_scatter(part_out, 'feat', scatter_dimension=1, tiled=True)  20.1 us
    dot_general x1, matrix products, shards(): part_in = jnp.dot(acts, proj_in, preferred_element_type=jnp.float32)  10.7 us
    dot_general x1, matrix products, shards(): part_out = jnp.dot(grads, proj_out, preferred_element_type=jnp.float32)  4.52 us
    dot_general x1, matrix products, outer_sum(): lax.dot_general(weighted, low_in, (((0,), (0,)), ((), ())), preferred_ele...  3.46 us
    ppermute x2, starting transfers between devices, shards(): lax.ppermute(full_in, 'feat', [(dev, dev ^ hop) for dev in range(4)])  3.39 us
  transfers between devices with their start and end apart: 4, of which 4 were waited for; matrix products, arithmetic and copies ran while one was open for 13% of the time, Pallas kernels for 0%

profile of v1, /device:TPU:0, one launch (start us, length us, event | category | flops | bytes accessed | tf_op | source)
XLA Modules:
  0.0 116.0 jit_solution(6427225293190634455)
XLA Ops:
  6.5 0.0 copy-start
  6.5 0.0 reduce-scatter.3.cloned.1.call-start
  6.5 1.9 %copy-done = bf16[768,2048]{1,0:T(8,128)(2,1)S(1)} copy-done((bf16[768,2048]{1,0:T(8,128)(2,1)S(1)}, bf16[768,2048]{1,0:T(8,128)(2,1)}, u32[]{:S(2)}) %copy-start) | copy-done | bytes 3145752
  8.4 4.5 %fusion.15 = f32[768,512]{1,0:T(8,128)} fusion(bf16[768,2048]{1,0:T(8,128)(2,1)S(1)} %copy-done, bf16[2048,512]{1,0:T(8,128)(2,1)} %param.9), kind=kOutput, calls=%fused_computation.23 | convolution fusion | flops 1610612736 | bytes 6815744 | tf_op jit(solution)/shard_map/dot_general | solution.py:24
  12.9 0.0 reduce-scatter.3.cloned.1.call-update
  13.0 0.0 reduce-scatter.5.cloned.1.call-start
  13.0 10.7 %fusion.16 = f32[768,512]{1,0:T(8,128)S(1)} fusion(bf16[768,7168]{1,0:T(8,128)(2,1)} %param.6, bf16[7168,512]{1,0:T(8,128)(2,1)} %param.8), kind=kOutput, calls=%fused_computation.24 | convolution fusion | flops 5637144576 | bytes 19922944 | tf_op jit(solution)/shard_map/dot_general | solution.py:23
  23.8 0.0 copy-start.1
  23.8 0.0 copy-start.2
  23.8 0.6 collective-permute-start
  24.3 3.0 %collective-permute-done = f32[768,512]{1,0:T(8,128)S(1)} collective-permute-done((f32[768,512]{1,0:T(8,128)S(1)}, f32[768,512]{1,0:T(8,128)S(1)}, u32[]{:S(2)}, u32[]{:S(2)}) %collective-permute-start) | collective-permute-done | bytes 1572896 | tf_op jit(solution)/shard_map/ppermute | solution.py:27
  27.4 1.5 %add.29 = f32[768,512]{1,0:T(8,128)} add(f32[768,512]{1,0:T(8,128)S(1)} %fusion.16, f32[768,512]{1,0:T(8,128)S(1)} %collective-permute-done) | non-fusion elementwise | flops 393216 | bytes 4718592 | tf_op jit(solution)/shard_map/add | solution.py:27
  28.9 2.8 %collective-permute-start.1 = (f32[768,512]{1,0:T(8,128)}, f32[768,512]{1,0:T(8,128)}, u32[]{:S(2)}, u32[]{:S(2)}) collective-permute-start(f32[768,512]{1,0:T(8,128)} %add.29), channel_id=1, source_target_pairs={{0,2},{1,3},{2,0},{3,1},{4,6},{5,7},{6,4},{7,5},{8,10},{9,11},{10,... | collective-permute-start | bytes 4718600 | tf_op jit(solution)/shard_map/ppermute | solution.py:27
  31.7 0.0 copy-done.1
  31.7 0.1 convert_reduce_fusion
  31.8 0.0 copy-done.2
  31.8 0.2 reduce-window.8
  32.0 0.3 convolution_convert_fusion
  32.3 20.1 %reduce-scatter.3.cloned.1.call-done = f32[768,128]{1,0:T(8,128)} async-done(((f32[768,512]{1,0:T(8,128)}), f32[768,128]{1,0:T(8,128)}) %reduce-scatter.3.cloned.1.call-update) | async-done | bytes 393232 | tf_op jit(solution)/shard_map/reduce_scatter | solution.py:28
  52.4 1.0 convert_element_type.17
  53.4 0.1 copy.9
  53.6 21.6 %collective-permute-done.1 = f32[768,512]{1,0:T(8,128)} collective-permute-done((f32[768,512]{1,0:T(8,128)}, f32[768,512]{1,0:T(8,128)}, u32[]{:S(2)}, u32[]{:S(2)}) %collective-permute-start.1) | collective-permute-done | bytes 1572896 | tf_op jit(solution)/shard_map/ppermute | solution.py:27
  75.2 3.5 %fusion.1 = f32[4,128,512]{2,1,0:T(8,128)} fusion(f32[768,512]{1,0:T(8,128)} %add.29, f32[768,512]{1,0:T(8,128)} %collective-permute-done.1, bf16[768,4]{0,1:T(4,128)(2,1)S(1)} %convolution_convert_fusion, bf16[768,128]{0,1:T(8,128)(2,1)S(1)} %copy.9), kind=kOutput, calls=%fused_computation.3 | convolution fusion | flops 403832832 | bytes 4397056 | tf_op jit(solution)/shard_map/dot_general | solution.py:13
  78.6 0.0 reduce-scatter.5.cloned.1.call-update
  78.6 0.1 select_reduce_fusion
  78.7 0.6 dynamic_slice.3
  80.0 27.4 %reduce-scatter.5.cloned.1.call-done = f32[1,128,512]{2,1,0:T(8,128)} async-done(((f32[4,128,512]{2,1,0:T(8,128)}), f32[1,128,512]{2,1,0:T(8,128)}) %reduce-scatter.5.cloned.1.call-update) | async-done | bytes 262160 | tf_op jit(solution)/shard_map/reduce_scatter | solution.py:46
  107.5 1.7 %broadcast_multiply_fusion = f32[1,128,512]{2,1,0:T(8,128)} fusion(f32[1,128,512]{2,1,0:T(8,128)} %reduce-scatter.5.cloned.1.call-done, f32[]{:T(128)} %bitcast.6), kind=kLoop, calls=%fused_computation.8 | loop fusion | flops 65536 | bytes 524292 | tf_op jit(solution)/shard_map/mul | solution.py:52
  (3 shorter events, 0.0 us)
Async XLA Ops:
  6.5 1.9 %copy-start = (bf16[768,2048]{1,0:T(8,128)(2,1)S(1)}, bf16[768,2048]{1,0:T(8,128)(2,1)}, u32[]{:S(2)}) copy-start(bf16[768,2048]{1,0:T(8,128)(2,1)} %param.7) | copy-start | bytes 9437188
  6.5 45.9 %reduce-scatter.3.cloned.1.call-start = ((), (), s32[]{:S(2)}) async-start(), calls=%async_computation.2 | async-start | bytes 1966080 | tf_op jit(solution)/shard_map/reduce_scatter | solution.py:28
  13.0 94.5 %reduce-scatter.5.cloned.1.call-start = ((), (), s32[]{:S(2)}) async-start(), calls=%async_computation.3 | async-start | bytes 1310720 | tf_op jit(solution)/shard_map/reduce_scatter | solution.py:46
  23.8 8.0 %copy-start.1 = (s32[4]{0:T(128)S(1)}, s32[4]{0:T(128)}, u32[]{:S(2)}) copy-start(s32[4]{0:T(128)} %param.11) | copy-start | bytes 52
  23.8 8.0 %copy-start.2 = (s32[4]{0:T(128)S(1)}, s32[4]{0:T(128)}, u32[]{:S(2)}) copy-start(s32[4]{0:T(128)} %param.10) | copy-start | bytes 52
  23.8 3.6 %collective-permute-start = (f32[768,512]{1,0:T(8,128)S(1)}, f32[768,512]{1,0:T(8,128)S(1)}, u32[]{:S(2)}, u32[]{:S(2)}) collective-permute-start(f32[768,512]{1,0:T(8,128)S(1)} %fusion.16), channel_id=1, source_target_pairs={{0,1},{1,0},{2,3},{3,2},{4,5},{5,4},{6,7},{7,6},{8,9},{9,8},{10,11... | collective-permute-start | bytes 4718600 | tf_op jit(solution)/shard_map/ppermute | solution.py:27
  28.9 46.3 %collective-permute-start.1 = (f32[768,512]{1,0:T(8,128)}, f32[768,512]{1,0:T(8,128)}, u32[]{:S(2)}, u32[]{:S(2)}) collective-permute-start(f32[768,512]{1,0:T(8,128)} %add.29), channel_id=1, source_target_pairs={{0,2},{1,3},{2,0},{3,1},{4,6},{5,7},{6,4},{7,5},{8,10},{9,11},{10,... | collective-permute-start | bytes 4718600 | tf_op jit(solution)/shard_map/ppermute | solution.py:27
Sparse Core Ops, SparseCore 0:
  13.1 39.2 reduce-scatter.2
  78.8 28.6 reduce-scatter.4
